TPU v7x, 32 devices: a whole 2x2x4 slice. The times are simulated.
32 devices in a mesh: grp: 4 (over x, core), fsdp: 8 (over z, y).
Axes of the slice: x: 2, y: 2, z: 4, core: 2. Of those that a mesh axis runs over, the one named last changes fastest.
Arguments:
- layer_input_rows: bfloat16 [16384, 8192], P(('grp', 'fsdp')), may hold values from -400 to 400, as said below
- input_norm_gain: bfloat16 [8192], replicated, may hold values from 0.5 to 1.5
- key_value_codes: int32 [8192, 256], P('fsdp'), may hold values from 0 to 65535
- block_scale_codes: int32 [256, 128], P('fsdp'), may hold values from -2147483648 to 2147483646
- outer_scale_codes: int32 [512], P('fsdp'), may hold values from 0 to 255
- adapter_down_factor: bfloat16 [8192, 64], replicated, may hold values from -0.0625 to 0.0625
- adapter_up_factor: bfloat16 [64, 1024], replicated, may hold values from -0.75 to 0.75
- target: bfloat16 [16384, 1024], P(('grp', 'fsdp')), may hold values from -18 to 18
Outputs:
- kv: bfloat16 [16384, 1024], P(('grp', 'fsdp'))
- loss: float32 [], replicated
Inputs may be any that keep to these rules, and one draw needn't show every extreme that they name: layer_input_rows rows and features carry varied scales.
All inputs are finite; a program needn't handle non-finite values.
Results may differ from a plain program's by a relative error of at most 0.0057.
Values may be sent and summed in bfloat16 or wider, within the bound.
A program may use at most 128 MiB of HBM per device.

v0:
```python
import jax
import jax.numpy as jnp
from jax import lax
from jax.sharding import PartitionSpec as P

adapter_scale = 0.25
epsilon = 1e-06
nf4_levels = (
    -1.0,
    -0.6961928009986877,
    -0.5250730514526367,
    -0.39491748809814453,
    -0.28444138169288635,
    -0.18477343022823334,
    -0.09105003625154495,
    0.0,
    0.07958029955625534,
    0.16093020141124725,
    0.24611230194568634,
    0.33791524171066284,
    0.44070982933044434,
    0.5626170039176941,
    0.7229568362236023,
    1.0,
)


def unpack_scales(code_words, outer_scale_codes, all_rows):
    per_row = code_words.size // all_rows
    flat = code_words.reshape(all_rows, per_row)
    shifts = jnp.arange(4, dtype=jnp.int32) * 8
    code_bytes = jnp.bitwise_and(jnp.right_shift(flat[:, :, None], shifts[None, None, :]), 255)
    code_bytes = code_bytes.reshape(all_rows, per_row * 4).astype(jnp.float32)
    group_rows = all_rows // outer_scale_codes.shape[0]
    second = jnp.exp2(outer_scale_codes.astype(jnp.float32) / 128.0 - 6.0)
    second = jnp.repeat(second, group_rows)
    return (code_bytes + 0.5) / 256.0 * second[:, None]


def decode_codes(words, absmax):
    height = words.shape[0]
    shifts = jnp.arange(4, dtype=jnp.int32) * 4
    nibbles = jnp.bitwise_and(jnp.right_shift(words[:, :, None], shifts[None, None, :]), 15)
    nibbles = nibbles.reshape(height, words.shape[1] * 4)
    values = jnp.zeros(nibbles.shape, jnp.float32)
    for number, level in enumerate(nf4_levels):
        values = jnp.where(nibbles == number, jnp.float32(level), values)
    width = values.shape[1]
    count = absmax.shape[1]
    scaled = values.reshape(height, count, width // count) * absmax[:, :, None]
    return scaled.reshape(height, width).astype(jnp.bfloat16)


def apply_input_norm(input_states, input_norm_gain):
    values = input_states.astype(jnp.float32)
    inverse = lax.rsqrt(jnp.mean(values * values, axis=1, keepdims=True) + epsilon)
    return (values * inverse * input_norm_gain.astype(jnp.float32)[None, :]).astype(jnp.bfloat16)


def per_device(
    layer_input_rows,
    input_norm_gain,
    key_value_codes,
    block_scale_codes,
    outer_scale_codes,
    adapter_down_factor,
    adapter_up_factor,
    target,
):
    normed_input = apply_input_norm(layer_input_rows, input_norm_gain)
    rows_dev = key_value_codes.shape[0]
    columns = key_value_codes.shape[1] * 4
    owned = decode_codes(
        key_value_codes, unpack_scales(block_scale_codes, outer_scale_codes, rows_dev)
    )
    frozen_output = jnp.dot(
        normed_input,
        lax.all_gather(owned, "fsdp", axis=0, tiled=True),
        preferred_element_type=jnp.float32,
    )
    adapter_output = jnp.dot(
        normed_input, adapter_down_factor, preferred_element_type=jnp.float32
    ).astype(jnp.bfloat16)
    precise_output = frozen_output + adapter_scale * jnp.dot(
        adapter_output, adapter_up_factor, preferred_element_type=jnp.float32
    )
    error_terms = precise_output - target.astype(jnp.float32)
    partial_value = jnp.sum(error_terms * error_terms) / (
        normed_input.shape[0] * lax.axis_size("fsdp") * columns
    )
    group_total = lax.psum(partial_value, "fsdp")
    loss = lax.psum(group_total, "grp")
    return (precise_output.astype(jnp.bfloat16), loss)


def solution(mesh):
    placed = (
        P(("grp", "fsdp"), None),
        P(),
        P("fsdp", None),
        P("fsdp", None),
        P("fsdp"),
        P(),
        P(),
        P(("grp", "fsdp"), None),
    )
    return jax.shard_map(
        per_device,
        mesh=mesh,
        in_specs=placed,
        out_specs=(P(("grp", "fsdp"), None), P()),
        check_vma=False,
    )
```

profile of v0, /device:TPU:0, one launch (start us, length us, event | category | flops | bytes accessed | tf_op | source)
XLA Modules:
  0.0 307.6 jit_solution(17579095723912490030)
XLA Ops:
  7.2 0.0 copy-start
  7.2 0.0 all-gather.2.cloned.1.call-start
  7.2 0.7 exponential_multiply_fusion
  8.0 0.1 shift_right_arithmetic.58
  8.1 0.1 broadcast_in_dim.75
  8.1 0.1 mul.80
  8.2 0.1 shift_right_arithmetic.51
  8.4 1.2 shift_right_arithmetic.54
  9.6 0.2 copy.11
  9.9 1.6 copy.10
  11.4 3.2 %shift_right_arithmetic.48 = s32[1024,256,4]{0,2,1:T(4,128)} broadcast(s32[1024,256]{0,1:T(8,128)S(1)} %copy.10), dimensions={0,1} | broadcast | bytes 5242880 | tf_op jit(solution)/shard_map/shift_right_arithmetic | solution.py:43
  14.6 5.3 %shift_right_arithmetic.49 = s32[1024,1024]{0,1:T(8,128)} reshape(s32[1024,256,4]{0,2,1:T(4,128)} %shift_right_arithmetic.48) | data formatting | bytes 8388608 | tf_op jit(solution)/shard_map/shift_right_arithmetic | solution.py:43
  19.9 0.1 add_multiply_fusion
  20.0 0.0 copy-start.1
  20.0 7.9 %fusion.3 = bf16[1024,1024]{0,1:T(8,128)(2,1)} fusion(s32[1024,1024]{0,1:T(8,128)} %shift_right_arithmetic.49, f32[1024,16]{0,1:T(8,128)S(1)} %add_multiply_fusion, s32[1024]{0:T(1024)S(1)} %shift_right_arithmetic.51), kind=kLoop, calls=%fused_computation.6 | loop fusion | flops 37748736 | bytes 6361088 | tf_op jit(solution)/shard_map/convert_element_type | solution.py:51
  27.9 0.0 all-gather.2.cloned.1.call-update
  27.9 0.0 copy-done.1
  27.9 0.0 copy-start.3
  27.9 5.1 %fusion = f32[512]{0:T(512)S(1)} fusion(bf16[512,8192]{1,0:T(8,128)(2,1)} %param.8), kind=kLoop, calls=%fused_computation.2 | loop fusion | flops 12582400 | bytes 8390656 | tf_op jit(solution)/shard_map/reduce_sum | solution.py:56
  33.1 0.0 copy-done
  33.1 0.0 copy-done.3
  33.1 0.0 copy-start.2
  33.1 8.0 %fusion.14 = f32[512,1024]{1,0:T(8,128)} fusion(bf16[64,1024]{1,0:T(8,128)(2,1)S(1)} %copy-done.3, bf16[8192,64]{0,1:T(8,128)(2,1)S(1)} %copy-done, bf16[512,8192]{1,0:T(8,128)(2,1)} %param.8, f32[8192]{0:T(1024)S(1)} %convert_element_type.32, f32[512]{0:T(512)S(1)} %add_rsqrt_fusion), kind=kOutput, calls=%fused_computation.13 | convolution fusion | flops 620789760 | bytes 11700224 | tf_op jit(solution)/shard_map/dot_general | solution.py:84
  41.1 217.0 %all-gather.2.cloned.1.call-done = bf16[8192,1024]{0,1:T(8,128)(2,1)} async-done(((bf16[1024,1024]{0,1:T(8,128)(2,1)}), bf16[8192,1024]{0,1:T(8,128)(2,1)}) %all-gather.2.cloned.1.call-update) | async-done | bytes 16777232 | tf_op jit(solution)/shard_map/all_gather | solution.py:78
  258.1 0.0 copy-done.2
  258.1 16.8 %multiply_reduce_fusion = (f32[]{:T(128)}, bf16[512,1024]{1,0:T(8,128)(2,1)}) fusion(bf16[512,1024]{1,0:T(8,128)(2,1)S(1)} %copy-done.2, f32[512,1024]{1,0:T(8,128)} %fusion.14, bf16[8192,1024]{0,1:T(8,128)(2,1)} %all-gather.2.cloned.1.call-done, bf16[512,8192]{1,0:T(8,128)(2,1)} %param.8, f32[8192]{0:T(1024)S(1)} %convert_element_type.32, ...), kind=kOutput, calls=%fused_computation.10 | convolution fusion | flops 8610381824 | bytes 29394948 | tf_op jit(solution)/shard_map/dot_general | solution.py:76
  275.5 19.0 %psum.14 = f32[]{:T(128)} all-reduce(f32[]{:T(128)S(6)} %div.21), channel_id=1, replica_groups=mesh['grp'=4,'fsdp'=8] {'fsdp'}, use_global_device_ids=true, to_apply=%region_2.3 | all-reduce | flops 1 | bytes 8 | tf_op jit(solution)/shard_map/psum | solution.py:91
  294.5 6.3 %psum.15 = f32[]{:T(128)} all-reduce(f32[]{:T(128)} %psum.14), channel_id=1, replica_groups=mesh['grp'=4,'fsdp'=8] {'grp'}, use_global_device_ids=true, to_apply=%region_3.4 | all-reduce | flops 1 | bytes 8 | tf_op jit(solution)/shard_map/psum | solution.py:92
  (8 shorter events, 0.1 us)
Async XLA Ops:
  7.2 25.9 %copy-start = (bf16[8192,64]{0,1:T(8,128)(2,1)S(1)}, bf16[8192,64]{0,1:T(8,128)(2,1)}, u32[]{:S(2)}) copy-start(bf16[8192,64]{0,1:T(8,128)(2,1)} %param.13) | copy-start | bytes 3145732
  7.2 250.9 %all-gather.2.cloned.1.call-start = ((), (), s32[]{:S(2)}) async-start(), calls=%async_computation | async-start | bytes 18874368 | tf_op jit(solution)/shard_map/all_gather | solution.py:78
  20.0 7.9 %copy-start.1 = (bf16[8192]{0:T(1024)(128)(2,1)S(1)}, bf16[8192]{0:T(1024)(128)(2,1)}, u32[]{:S(2)}) copy-start(bf16[8192]{0:T(1024)(128)(2,1)} %param.9) | copy-start | bytes 49156
  27.9 5.2 %copy-start.3 = (bf16[64,1024]{1,0:T(8,128)(2,1)S(1)}, bf16[64,1024]{1,0:T(8,128)(2,1)}, u32[]{:S(2)}) copy-start(bf16[64,1024]{1,0:T(8,128)(2,1)} %param.14) | copy-start | bytes 393220
  33.1 225.0 %copy-start.2 = (bf16[512,1024]{1,0:T(8,128)(2,1)S(1)}, bf16[512,1024]{1,0:T(8,128)(2,1)}, u32[]{:S(2)}) copy-start(bf16[512,1024]{1,0:T(8,128)(2,1)} %param.15) | copy-start | bytes 3145732
Sparse Core Ops, SparseCore 0:
  28.0 229.9 all-gather.1
where the time goes:
time: 308 us
  waiting for transfers between devices  217 us (70%)
  blocking collectives  25.3 us (8%)
  matrix products  24.8 us (8%)
  between operations  14.8 us (5%)
  other arithmetic  13.9 us (5%)
  local copies, waits for them, and re-layouts  11.9 us (4%)
    all_gather x1, waiting for transfers between devices, per_device(): lax.all_gather(owned, 'fsdp', axis=0, tiled=True)  217 us
    psum x1, blocking collectives, per_device(): group_total = lax.psum(partial_value, 'fsdp')  19 us
    dot_general x1, matrix products, per_device(): jnp.dot(normed_input, lax.all_gather(owned, 'fsdp', axis=0, tiled=True),...  16.8 us
    shift_right_arithmetic x4, local copies, waits for them, and re-layouts, decode_codes(): jnp.right_shift(words[:, :, None], shifts[None, None, :])  8.59 us
    dot_general x1, matrix products, per_device(): jnp.dot(adapter_output, adapter_up_factor, preferred_element_type=jnp.flo...  7.95 us
    convert_element_type x1, other arithmetic, decode_codes(): return scaled.reshape(height, width).astype(jnp.bfloat16)  7.88 us
    psum x1, blocking collectives, per_device(): loss = lax.psum(group_total, 'grp')  6.27 us
  transfers between devices with their start and end apart: 1, of which 1 were waited for; matrix products, arithmetic and copies ran while one was open for 4% of the time, Pallas kernels for 0%

commit v1 on v0

v1 whole, which is shorter than its diff:
```python
import functools

import jax
import jax.numpy as jnp
from jax import lax
from jax.experimental import pallas as pl
from jax.experimental.pallas import tpu as pltpu
from jax.sharding import PartitionSpec as P

adapter_scale = 0.25
epsilon = 1e-06
nf4_levels = (
    -1.0,
    -0.6961928009986877,
    -0.5250730514526367,
    -0.39491748809814453,
    -0.28444138169288635,
    -0.18477343022823334,
    -0.09105003625154495,
    0.0,
    0.07958029955625534,
    0.16093020141124725,
    0.24611230194568634,
    0.33791524171066284,
    0.44070982933044434,
    0.5626170039176941,
    0.7229568362236023,
    1.0,
)
MESH = pl.DeviceIdType.MESH


def nibble_levels(words, plane):
    values = [jnp.float32(level) for level in nf4_levels]
    for bit in range(4):
        is_set = jnp.bitwise_and(words, 1 << (4 * plane + bit)) != 0
        values = [
            jnp.where(is_set, values[2 * i + 1], values[2 * i])
            for i in range(len(values) // 2)
        ]
    return values[0]


def kernel(
    layers,
    x_hbm,
    gain_ref,
    codes_ref,
    scales_ref,
    outer_ref,
    down_hbm,
    up_ref,
    target_hbm,
    out_ref,
    loss_ref,
    x_ref,
    weight_ref,
    acc_ref,
    target_ref,
    down_ref,
    spread_ref,
    scale_ref,
    local_sem,
    z_send,
    x_send,
    y_send,
    own_send,
    core_send,
    link_recv,
    core_recv,
):
    g = lax.axis_index("grp")
    f = lax.axis_index("fsdp")
    cx, cc = g // 2, g % 2
    cl, cy = f // 2, f % 2
    tokens, width = x_ref.shape
    columns = acc_ref.shape[1]
    rows = codes_ref.shape[0]
    half = rows // 2
    piece = half // 4

    sibling = (cx * 2 + 1 - cc, f)
    x_peer = ((1 - cx) * 2 + cc, f)
    y_peer = (g, cl * 2 + 1 - cy)

    def z_peer(step):
        return (g, (cl + step) * 2 + cy)

    part = tokens // 4
    x_copies = [
        pltpu.make_async_copy(
            x_hbm.at[pl.ds(p * part, part)], x_ref.at[pl.ds(p * part, part)], local_sem.at[p]
        )
        for p in range(4)
    ]
    target_copy = pltpu.make_async_copy(target_hbm, target_ref, local_sem.at[4])
    down_copy = pltpu.make_async_copy(down_hbm, down_ref, local_sem.at[5])
    for copy in x_copies:
        copy.start()
    down_copy.start()
    target_copy.start()

    barrier = pltpu.get_barrier_semaphore()
    for peer in (sibling, x_peer, y_peer):
        pl.semaphore_signal(barrier, inc=1, device_id=peer, device_id_type=MESH)

    @pl.when(cl > 0)
    def _():
        pl.semaphore_signal(barrier, inc=1, device_id=z_peer(-1), device_id_type=MESH)

    @pl.when(cl < layers - 1)
    def _():
        pl.semaphore_signal(barrier, inc=1, device_id=z_peer(1), device_id_type=MESH)

    def mirror(px, j):
        return j + px * (3 - 2 * j)

    def chunk(layer, y, c, q):
        start = ((layer * 2 + y) * 2 + c) * half + q * piece
        return weight_ref.at[pl.ds(pl.multiple_of(start, piece), piece)]

    def slot(layer, y, q):
        return (layer * 2 + y) * 4 + q

    def link_copy(layer, y, q, send_sem, peer):
        ref = chunk(layer, y, cc, q)
        return pltpu.make_async_remote_copy(
            src_ref=ref,
            dst_ref=ref,
            send_sem=send_sem,
            recv_sem=link_recv.at[slot(layer, y, q)],
            device_id=peer,
            device_id_type=MESH,
        )

    def z_copy(layer, j, step):
        sem = z_send.at[(1 + step) // 2 * (layers * 3) + layer * 3 + j]
        return link_copy(layer, cy, mirror(cx, j), sem, z_peer(step))

    def xz_copy(layer):
        return link_copy(layer, cy, mirror(cx, 0), x_send.at[layer * 3], x_peer)

    def xy_copy(layer, j):
        return link_copy(layer, 1 - cy, mirror(cx, j), x_send.at[layer * 3 + 1 + j], x_peer)

    def y_copy(layer, j):
        return link_copy(layer, cy, mirror(cx, j), y_send.at[layer * 2 + j], y_peer)

    def own_copy(k):
        return link_copy(cl, cy, k, own_send.at[k], y_peer)

    def core_copy(layer, y, q):
        ref = chunk(layer, y, cc, q)
        place = slot(layer, y, q)
        return pltpu.make_async_remote_copy(
            src_ref=ref,
            dst_ref=ref,
            send_sem=core_send.at[place],
            recv_sem=core_recv.at[place],
            device_id=sibling,
            device_id_type=MESH,
        )

    def arrived(layer, y, q):
        ref = chunk(layer, y, cc, q)
        pltpu.make_async_copy(ref, ref, link_recv.at[slot(layer, y, q)]).wait()

    def core_arrived(layer, y, q):
        ref = chunk(layer, y, 1 - cc, q)
        pltpu.make_async_copy(ref, ref, core_recv.at[slot(layer, y, q)]).wait()

    words = codes_ref.shape[1]
    lanes = scales_ref.shape[1]
    per_row = scales_ref.shape[0] * lanes // rows
    line = rows // scales_ref.shape[0]
    row = lax.broadcasted_iota(jnp.int32, (rows, lanes), 0)
    lane = lax.broadcasted_iota(jnp.int32, (rows, lanes), 1)
    mine = lane // per_row == row % line
    place = lax.broadcasted_iota(jnp.int32, (lanes, words), 0)
    word = lax.broadcasted_iota(jnp.int32, (lanes, words), 1)
    run = words // (4 * per_row)
    code = jnp.zeros((rows, words), jnp.float32)
    scale_words = jnp.concatenate(
        [
            jnp.broadcast_to(scales_ref[pl.ds(i, 1), :], (line, lanes))
            for i in range(scales_ref.shape[0])
        ],
        axis=0,
    )
    for byte in range(4):
        value = jnp.bitwise_and(jnp.right_shift(scale_words, 8 * byte), 255)
        value = jnp.where(mine, value.astype(jnp.float32), 0.0).astype(jnp.bfloat16)
        pick = (place % per_row == word // (4 * run)) & ((word // run) % 4 == byte)
        code += jnp.dot(
            value,
            jnp.where(pick, 1.0, 0.0).astype(jnp.bfloat16),
            preferred_element_type=jnp.float32,
        )
    outer_count = outer_ref.shape[1]
    outer_rows = rows // outer_count
    outer_row = lax.broadcasted_iota(jnp.int32, (rows, outer_count), 0)
    outer_lane = lax.broadcasted_iota(jnp.int32, (rows, outer_count), 1)
    second = jnp.sum(
        jnp.where(
            outer_row // outer_rows == outer_lane, outer_ref[...].astype(jnp.float32), 0.0
        ),
        axis=1,
        keepdims=True,
    )
    second = jnp.exp2(second / 128.0 - 6.0)
    scale_ref[...] = (code + 0.5) / 256.0 * second

    deep = lax.broadcasted_iota(jnp.int32, spread_ref.shape, 0)
    wide = lax.broadcasted_iota(jnp.int32, spread_ref.shape, 1)
    spread_ref[...] = jnp.where(
        (deep % 128) * 4 + deep // 128 == wide, 1.0, 0.0
    ).astype(jnp.bfloat16)

    def decode(start):
        start = pl.multiple_of(start, piece)
        for h in range(words // 128):
            span = pl.ds(h * 128, 128)
            code_words = codes_ref[pl.ds(start, piece), span]
            scale = scale_ref[pl.ds(start, piece), span]
            planes = [
                (nibble_levels(code_words, plane) * scale).astype(jnp.bfloat16)
                for plane in range(4)
            ]
            ordered = jnp.dot(
                jnp.concatenate(planes, axis=1),
                spread_ref[...],
                preferred_element_type=jnp.float32,
            )
            weight_ref[
                pl.ds(pl.multiple_of(f * rows + start, piece), piece), pl.ds(h * 512, 512)
            ] = ordered.astype(jnp.bfloat16)

    decode(cc * half + mirror(cx, 0) * piece)
    pl.semaphore_wait(
        barrier, 3 + (cl > 0).astype(jnp.int32) + (cl < layers - 1).astype(jnp.int32)
    )

    def first_sends(j):
        @pl.when(cl > 0)
        def _():
            z_copy(cl, j, -1).start()

        @pl.when(cl < layers - 1)
        def _():
            z_copy(cl, j, 1).start()

    def rest(j, carry):
        decode(cc * half + mirror(cx, j) * piece)
        first_sends(j - 1)
        return carry

    lax.fori_loop(1, 4, rest, 0)
    own_copy(0).start()
    for k in range(layers, 4):
        own_copy(k).start()

    def other(j, carry):
        decode((1 - cc) * half + j * piece)
        return carry

    lax.fori_loop(0, 4, other, 0)

    block = min(16, part)
    tile = min(1024, width)

    def normalize(p):
        x_copies[p].wait()

        def some(i, carry):
            at = pl.ds(pl.multiple_of(p * part + i * block, block), block)
            total = jnp.zeros((block, 128), jnp.float32)
            for t in range(width // tile):
                v = x_ref[at, pl.ds(t * tile, tile)].astype(jnp.float32)
                v = v * v
                for k in range(tile // 128):
                    total += v[:, k * 128 : (k + 1) * 128]
            inverse = lax.rsqrt(jnp.sum(total, axis=1, keepdims=True) / width + epsilon)
            for t in range(width // tile):
                span = pl.ds(t * tile, tile)
                v = x_ref[at, span].astype(jnp.float32)
                x_ref[at, span] = (v * inverse * gain_ref[:, span].astype(jnp.float32)).astype(
                    jnp.bfloat16
                )
            return carry

        lax.fori_loop(0, part // block, some, 0)

    def adapter():
        down_copy.wait()
        low = jnp.dot(x_ref[...], down_ref[...], preferred_element_type=jnp.float32)
        acc_ref[...] = adapter_scale * jnp.dot(
            low.astype(jnp.bfloat16), up_ref[...], preferred_element_type=jnp.float32
        )

    across = min(256, columns)

    def multiply(layer, y):
        at = pl.ds(pl.multiple_of((layer * 2 + y) * rows, rows), rows)

        def some(n, carry):
            cols = pl.ds(pl.multiple_of(n * across, across), across)
            acc_ref[:, cols] += jnp.dot(
                x_ref[:, at], weight_ref[at, cols], preferred_element_type=jnp.float32
            )
            return carry

        lax.fori_loop(0, columns // across, some, 0)

    def multiply_arrived(layer, y):
        for q in range(4):
            core_arrived(layer, y, q)
        multiply(layer, y)

    def both(s, act):
        for step in (-1, 1):
            layer = cl + step * s
            pl.when((layer >= 0) & (layer < layers))(functools.partial(act, layer, step))

    def z_event(s, j):
        def act(layer, step):
            arrived(layer, cy, mirror(cx, j))
            onward = cl - step

            @pl.when((onward >= 0) & (onward < layers))
            def _():
                z_copy(layer, j, -step).start()

            if j == 0:
                xz_copy(layer).start()
            if j < 2:
                y_copy(layer, j).start()
            core_copy(layer, cy, mirror(cx, j)).start()

        both(s, act)

    def y_event(s, j):
        def act(layer, step):
            q = mirror(cx, j)
            arrived(layer, 1 - cy, q)
            xy_copy(layer, j).start()
            core_copy(layer, 1 - cy, q).start()

        both(s, act)

    def xz_event(s):
        def act(layer, step):
            q = mirror(1 - cx, 0)
            arrived(layer, cy, q)
            core_copy(layer, cy, q).start()

        both(s, act)

    def xy_event(s, j):
        def act(layer, step):
            q = mirror(1 - cx, j)
            arrived(layer, 1 - cy, q)
            core_copy(layer, 1 - cy, q).start()

        both(s, act)

    def own_event(k):
        arrived(cl, 1 - cy, k)
        core_copy(cl, 1 - cy, k).start()

    def one_step(s, carry):
        z_event(s, 0)
        pl.when(s <= 4)(lambda: own_event(s - 1))

        @pl.when(s > 1)
        def _():
            xy_event(s - 1, 1)
            both(s - 1, lambda layer, step: multiply_arrived(layer, cy))

        @pl.when(s == 1)
        def _():
            normalize(0)
            normalize(1)

        z_event(s, 1)
        y_event(s, 0)
        xz_event(s)

        @pl.when(s > 1)
        def _():
            both(s - 1, lambda layer, step: multiply_arrived(layer, 1 - cy))

        @pl.when(s == 1)
        def _():
            normalize(2)
            normalize(3)

        z_event(s, 2)
        pl.when(s < 4)(lambda: own_copy(s).start())
        y_event(s, 1)
        xy_event(s, 0)

        @pl.when(s == 1)
        def _():
            adapter()
            multiply(cl, cy)

        return carry

    lax.fori_loop(1, layers, one_step, 0)
    for k in range(min(layers - 1, 4), 4):
        own_event(k)
    xy_event(layers - 1, 1)
    both(layers - 1, lambda layer, step: multiply_arrived(layer, cy))
    multiply_arrived(cl, 1 - cy)
    both(layers - 1, lambda layer, step: multiply_arrived(layer, 1 - cy))

    target_copy.wait()
    loss_ref[...] = jnp.zeros_like(loss_ref)

    def finish(i, carry):
        at = pl.ds(pl.multiple_of(i * block, block), block)
        exact = acc_ref[at, :]
        out_ref[at, :] = exact.astype(jnp.bfloat16)
        error = exact - target_ref[at, :].astype(jnp.float32)
        error = error * error
        total = jnp.zeros((block, 128), jnp.float32)
        for k in range(columns // 128):
            total += error[:, k * 128 : (k + 1) * 128]
        for k in range(block // 8):
            loss_ref[...] += total[k * 8 : (k + 1) * 8]
        return carry

    lax.fori_loop(0, tokens // block, finish, 0)

    for j in range(3):
        for step in (-1, 1):

            @pl.when((cl + step >= 0) & (cl + step < layers))
            def _():
                z_copy(cl, j, step).wait_send()

    def sent(s, carry):
        def act(layer, step):
            onward = cl - step

            @pl.when((onward >= 0) & (onward < layers))
            def _():
                for j in range(3):
                    z_copy(layer, j, -step).wait_send()

            xz_copy(layer).wait_send()
            for j in range(2):
                y_copy(layer, j).wait_send()
                xy_copy(layer, j).wait_send()
            for q in range(4):
                core_copy(layer, cy, q).wait_send()
                core_copy(layer, 1 - cy, q).wait_send()

        both(s, act)
        return carry

    lax.fori_loop(1, layers, sent, 0)
    for k in range(4):
        own_copy(k).wait_send()
        core_copy(cl, 1 - cy, k).wait_send()


def per_device(fsdp, x, gain, codes, scales, outer, down, up, target):
    tokens, width = x.shape
    columns = up.shape[1]
    rows = codes.shape[0]
    layers = fsdp // 2
    vmem = pl.BlockSpec(memory_space=pltpu.VMEM)
    anywhere = pl.BlockSpec(memory_space=pl.ANY)
    dma = pltpu.SemaphoreType.DMA
    kv, squares = pl.pallas_call(
        functools.partial(kernel, layers),
        out_shape=(
            jax.ShapeDtypeStruct((tokens, columns), jnp.bfloat16),
            jax.ShapeDtypeStruct((8, 128), jnp.float32),
        ),
        in_specs=[anywhere, vmem, vmem, vmem, vmem, anywhere, vmem, anywhere],
        out_specs=(vmem, vmem),
        scratch_shapes=[
            pltpu.VMEM((tokens, width), jnp.bfloat16),
            pltpu.VMEM((width, columns), jnp.bfloat16),
            pltpu.VMEM((tokens, columns), jnp.float32),
            pltpu.VMEM((tokens, columns), jnp.bfloat16),
            pltpu.VMEM(down.shape, jnp.bfloat16),
            pltpu.VMEM((512, 512), jnp.bfloat16),
            pltpu.VMEM(codes.shape, jnp.float32),
            dma((6,)),
            dma((2 * layers * 3,)),
            dma((layers * 3,)),
            dma((layers * 2,)),
            dma((4,)),
            dma((layers * 8,)),
            dma((layers * 8,)),
            dma((layers * 8,)),
        ],
        compiler_params=pltpu.CompilerParams(
            collective_id=0, has_side_effects=True, vmem_limit_bytes=60 * 1024 * 1024
        ),
    )(x, gain.reshape(1, width), codes, scales, outer.reshape(1, -1), down, up, target)
    partial_value = jnp.sum(squares) / (tokens * fsdp * columns)
    return kv, lax.psum(partial_value, ("grp", "fsdp"))


def solution(mesh):
    placed = (
        P(("grp", "fsdp"), None),
        P(),
        P("fsdp", None),
        P("fsdp", None),
        P("fsdp"),
        P(),
        P(),
        P(("grp", "fsdp"), None),
    )
    return jax.shard_map(
        functools.partial(per_device, mesh.shape["fsdp"]),
        mesh=mesh,
        in_specs=placed,
        out_specs=(P(("grp", "fsdp"), None), P()),
        check_vma=False,
    )
```

time: 308 us -> 132 us (0.43)
  waiting for transfers between devices: 217 us -> 0 us
  Pallas kernels: 0 us -> 83.3 us
  matrix products: 24.8 us -> 0 us
  between operations: 14.8 us -> 1.29 us
  blocking collectives: 25.3 us -> 38.7 us
  other arithmetic: 13.9 us -> 1.29 us
  local copies, waits for them, and re-layouts: 11.9 us -> 6.39 us
    all_gather x1 -> x0, waiting for transfers between devices: 217 us -> none  [per_device(): lax.all_gather(owned, 'fsdp', axis=0, tiled=True)]
    pallas_call x0 -> x1, Pallas kernels: none -> 83.3 us  [per_device(): pl.pallas_call(functools.partial(kernel, layers), out_shape=(jax.ShapeDty...]
    dot_general x2 -> x0, matrix products: 24.8 us -> none  [the longest x1 16.8 us: per_device(): jnp.dot(normed_input, lax.all_gather(owned, 'fsdp', axis=0, tiled=True),...]
    psum x2 -> x1, blocking collectives: 25.3 us -> 38.7 us  [per_device(): return (kv, lax.psum(partial_value, ('grp', 'fsdp')))]
    shift_right_arithmetic x10 -> x0, local copies, waits for them, and re-layouts: 10.2 us -> none  [the longest x4 8.59 us: decode_codes(): jnp.right_shift(words[:, :, None], shifts[None, None, :])]
    convert_element_type x2 -> x0, other arithmetic: 7.89 us -> none  [the longest x1 7.88 us: decode_codes(): return scaled.reshape(height, width).astype(jnp.bfloat16)]
    reduce_sum x1, other arithmetic: 5.14 us -> 1.29 us  [per_device(): partial_value = jnp.sum(squares) / (tokens * fsdp * columns)]
    unnamed x9 -> x2, local copies, waits for them, and re-layouts: 1.59 us -> 5.04 us
  transfers between devices with their start and end apart: 1 -> 0, of which waited for: 1 -> 0; matrix products, arithmetic and copies ran while one was open for 4% -> 0% of each run, Pallas kernels for 0% -> 0%
where the time goes in v1:
time: 132 us; the launch traced here: 131 us
  Pallas kernels  83.3 us (63%)
  blocking collectives  38.7 us (29%)
  local copies, waits for them, and re-layouts  6.39 us (5%)
    pallas_call x1, Pallas kernels, per_device(): pl.pallas_call(functools.partial(kernel, layers), out_shape=(jax.ShapeDty...  83.3 us
    psum x1, blocking collectives, per_device(): return (kv, lax.psum(partial_value, ('grp', 'fsdp')))  38.7 us
    unnamed x2, local copies, waits for them, and re-layouts  5.04 us

profile of v1, /device:TPU:0, one launch (start us, length us, event | category | flops | bytes accessed | tf_op | source)
XLA Modules:
  0.0 131.0 jit_solution(16605868003587576911)
XLA Ops:
  0.6 1.4 %reshape.10.gain_ref = bf16[1,8192]{1,0:T(2,128)(2,1)} reshape(bf16[8192]{0:T(1024)(128)(2,1)} %param.9) | data formatting | bytes 32768 | tf_op jit(solution)/shard_map/reshape | solution.py:504
  2.0 2.8 %copy.10.down_hbm = bf16[8192,64]{1,0:T(8,128)(2,1)} copy(bf16[8192,64]{0,1:T(8,128)(2,1)} %param.13) | data formatting | bytes 2097152 | tf_op args[5]
  4.8 83.3 %shard_map.95 = (bf16[512,1024]{1,0:T(8,128)(2,1)}, f32[8,128]{1,0:T(8,128)}) custom-call(bf16[512,8192]{1,0:T(8,128)(2,1)} %x_hbm.1, bf16[1,8192]{1,0:T(2,128)(2,1)} %reshape.10.gain_ref, s32[1024,256]{1,0:T(8,128)} %codes_ref.1, s32[32,128]{1,0:T(8,128)} %scales_ref.1, s32[1,64]{1,0:T(1,128)} %bitcast.1, bf16[8192,64]{1,0:T(8,128)(2,1)} %copy.10.down_hbm, ...), custom_call_target="tpu_custom_call" | custom-call | tf_op jit(solution)/shard_map/pallas_call | solution.py:476
  88.1 1.3 reduce_sum.9
  90.0 38.7 %psum.7 = f32[]{:T(128)} all-reduce(f32[]{:T(128)S(6)} %div.3), channel_id=1, replica_groups=mesh['grp'=4,'fsdp'=8] {'grp','fsdp'}, use_global_device_ids=true, to_apply=%region_1.0 | all-reduce | flops 1 | bytes 8 | tf_op jit(solution)/shard_map/psum | solution.py:506
  128.8 2.3 %copy.12 = bf16[512,1024]{1,0:T(8,128)(2,1)} copy(bf16[512,1024]{1,0:T(8,128)(2,1)} %get-tuple-element.8) | data formatting | bytes 2097152

commit v2 on v1

--- a/solution.py
+++ b/solution.py
@@ -60,6 +60,9 @@
     down_ref,
     spread_ref,
     scale_ref,
+    wide_gain_ref,
+    plane_ref,
+    line_ref,
     local_sem,
     z_send,
     x_send,
@@ -68,6 +71,10 @@
     core_send,
     link_recv,
     core_recv,
+    plane_send,
+    plane_recv,
+    line_send,
+    line_recv,
 ):
     g = lax.axis_index("grp")
     f = lax.axis_index("fsdp")
@@ -101,16 +108,23 @@
     target_copy.start()
 
     barrier = pltpu.get_barrier_semaphore()
-    for peer in (sibling, x_peer, y_peer):
-        pl.semaphore_signal(barrier, inc=1, device_id=peer, device_id_type=MESH)
-
-    @pl.when(cl > 0)
-    def _():
-        pl.semaphore_signal(barrier, inc=1, device_id=z_peer(-1), device_id_type=MESH)
-
-    @pl.when(cl < layers - 1)
-    def _():
-        pl.semaphore_signal(barrier, inc=1, device_id=z_peer(1), device_id_type=MESH)
+    spot = (cx * 2 + cc) * 2 + cy
+
+    def plane_peer(i):
+        to = (spot + i) % 8
+        return (to // 2, cl * 2 + to % 2)
+
+    def line_peer(i):
+        return (g, (cl + i) % layers * 2 + cy)
+
+    for i in range(1, 8):
+        pl.semaphore_signal(barrier, inc=1, device_id=plane_peer(i), device_id_type=MESH)
+
+    def greet(i, carry):
+        pl.semaphore_signal(barrier, inc=1, device_id=line_peer(i), device_id_type=MESH)
+        return carry
+
+    lax.fori_loop(1, layers, greet, 0)
 
     def mirror(px, j):
         return j + px * (3 - 2 * j)
@@ -147,7 +161,7 @@
         return link_copy(layer, cy, mirror(cx, j), y_send.at[layer * 2 + j], y_peer)
 
     def own_copy(k):
-        return link_copy(cl, cy, k, own_send.at[k], y_peer)
+        return link_copy(cl, cy, mirror(cx, k), own_send.at[k], y_peer)
 
     def core_copy(layer, y, q):
         ref = chunk(layer, y, cc, q)
@@ -168,6 +182,8 @@
     def core_arrived(layer, y, q):
         ref = chunk(layer, y, 1 - cc, q)
         pltpu.make_async_copy(ref, ref, core_recv.at[slot(layer, y, q)]).wait()
+
+    wide_gain_ref[...] = gain_ref[...].astype(jnp.float32)
 
     words = codes_ref.shape[1]
     lanes = scales_ref.shape[1]
@@ -236,9 +252,7 @@
             ] = ordered.astype(jnp.bfloat16)
 
     decode(cc * half + mirror(cx, 0) * piece)
-    pl.semaphore_wait(
-        barrier, 3 + (cl > 0).astype(jnp.int32) + (cl < layers - 1).astype(jnp.int32)
-    )
+    pl.semaphore_wait(barrier, 7 + layers - 1)
 
     def first_sends(j):
         @pl.when(cl > 0)
@@ -248,6 +262,8 @@
         @pl.when(cl < layers - 1)
         def _():
             z_copy(cl, j, 1).start()
+
+        pl.when(j == 0)(lambda: own_copy(0).start())
 
     def rest(j, carry):
         decode(cc * half + mirror(cx, j) * piece)
@@ -255,7 +271,6 @@
         return carry
 
     lax.fori_loop(1, 4, rest, 0)
-    own_copy(0).start()
     for k in range(layers, 4):
         own_copy(k).start()
 
@@ -280,19 +295,22 @@
                 for k in range(tile // 128):
                     total += v[:, k * 128 : (k + 1) * 128]
             inverse = lax.rsqrt(jnp.sum(total, axis=1, keepdims=True) / width + epsilon)
-            for t in range(width // tile):
-                span = pl.ds(t * tile, tile)
+            for t in range(width // 128):
+                span = pl.ds(t * 128, 128)
                 v = x_ref[at, span].astype(jnp.float32)
-                x_ref[at, span] = (v * inverse * gain_ref[:, span].astype(jnp.float32)).astype(
-                    jnp.bfloat16
-                )
+                x_ref[at, span] = (v * inverse * wide_gain_ref[pl.ds(t, 1), :]).astype(jnp.bfloat16)
             return carry
 
         lax.fori_loop(0, part // block, some, 0)
 
     def adapter():
         down_copy.wait()
-        low = jnp.dot(x_ref[...], down_ref[...], preferred_element_type=jnp.float32)
+        low = lax.dot_general(
+            x_ref[...],
+            down_ref[...],
+            (((1,), (1,)), ((), ())),
+            preferred_element_type=jnp.float32,
+        )
         acc_ref[...] = adapter_scale * jnp.dot(
             low.astype(jnp.bfloat16), up_ref[...], preferred_element_type=jnp.float32
         )
@@ -364,8 +382,9 @@
         both(s, act)
 
     def own_event(k):
-        arrived(cl, 1 - cy, k)
-        core_copy(cl, 1 - cy, k).start()
+        q = mirror(cx, k)
+        arrived(cl, 1 - cy, q)
+        core_copy(cl, 1 - cy, q).start()
 
     def one_step(s, carry):
         z_event(s, 0)
@@ -407,15 +426,15 @@
         return carry
 
     lax.fori_loop(1, layers, one_step, 0)
+    both(layers - 1, lambda layer, step: multiply_arrived(layer, cy))
     for k in range(min(layers - 1, 4), 4):
         own_event(k)
     xy_event(layers - 1, 1)
-    both(layers - 1, lambda layer, step: multiply_arrived(layer, cy))
     multiply_arrived(cl, 1 - cy)
     both(layers - 1, lambda layer, step: multiply_arrived(layer, 1 - cy))
 
     target_copy.wait()
-    loss_ref[...] = jnp.zeros_like(loss_ref)
+    plane_ref[spot] = jnp.zeros((8, 128), jnp.float32)
 
     def finish(i, carry):
         at = pl.ds(pl.multiple_of(i * block, block), block)
@@ -427,7 +446,7 @@
         for k in range(columns // 128):
             total += error[:, k * 128 : (k + 1) * 128]
         for k in range(block // 8):
-            loss_ref[...] += total[k * 8 : (k + 1) * 8]
+            plane_ref[spot] += total[k * 8 : (k + 1) * 8]
         return carry
 
     lax.fori_loop(0, tokens // block, finish, 0)
@@ -463,6 +482,52 @@
     for k in range(4):
         own_copy(k).wait_send()
         core_copy(cl, 1 - cy, k).wait_send()
+
+    def plane_copy(i):
+        return pltpu.make_async_remote_copy(
+            src_ref=plane_ref.at[spot],
+            dst_ref=plane_ref.at[spot],
+            send_sem=plane_send.at[i],
+            recv_sem=plane_recv.at[spot],
+            device_id=plane_peer(i),
+            device_id_type=MESH,
+        )
+
+    def line_copy(i):
+        return pltpu.make_async_remote_copy(
+            src_ref=line_ref.at[cl],
+            dst_ref=line_ref.at[cl],
+            send_sem=line_send.at[i],
+            recv_sem=line_recv.at[cl],
+            device_id=line_peer(i),
+            device_id_type=MESH,
+        )
+
+    def landed(ref, sem):
+        pltpu.make_async_copy(ref, ref, sem).wait()
+
+    for i in range(1, 8):
+        plane_copy(i).start()
+    for i in range(1, 8):
+        source = (spot + i) % 8
+        landed(plane_ref.at[source], plane_recv.at[source])
+    line_ref[cl] = jnp.sum(plane_ref[...], axis=0)
+    for i in range(1, 8):
+        plane_copy(i).wait_send()
+
+    def to_line(i, carry):
+        line_copy(i).start()
+        return carry
+
+    def from_line(i, carry):
+        source = (cl + i) % layers
+        landed(line_ref.at[source], line_recv.at[source])
+        line_copy(i).wait_send()
+        return carry
+
+    lax.fori_loop(1, layers, to_line, 0)
+    lax.fori_loop(1, layers, from_line, 0)
+    loss_ref[0, 0] = jnp.sum(line_ref[...]) / (tokens * layers * 2 * columns)
 
 
 def per_device(fsdp, x, gain, codes, scales, outer, down, up, target):
@@ -473,22 +538,25 @@
     vmem = pl.BlockSpec(memory_space=pltpu.VMEM)
     anywhere = pl.BlockSpec(memory_space=pl.ANY)
     dma = pltpu.SemaphoreType.DMA
-    kv, squares = pl.pallas_call(
+    kv, loss = pl.pallas_call(
         functools.partial(kernel, layers),
         out_shape=(
             jax.ShapeDtypeStruct((tokens, columns), jnp.bfloat16),
-            jax.ShapeDtypeStruct((8, 128), jnp.float32),
+            jax.ShapeDtypeStruct((1, 1), jnp.float32),
         ),
         in_specs=[anywhere, vmem, vmem, vmem, vmem, anywhere, vmem, anywhere],
-        out_specs=(vmem, vmem),
+        out_specs=(vmem, pl.BlockSpec(memory_space=pltpu.SMEM)),
         scratch_shapes=[
             pltpu.VMEM((tokens, width), jnp.bfloat16),
             pltpu.VMEM((width, columns), jnp.bfloat16),
             pltpu.VMEM((tokens, columns), jnp.float32),
             pltpu.VMEM((tokens, columns), jnp.bfloat16),
-            pltpu.VMEM(down.shape, jnp.bfloat16),
+            pltpu.VMEM(down.shape[::-1], jnp.bfloat16),
             pltpu.VMEM((512, 512), jnp.bfloat16),
             pltpu.VMEM(codes.shape, jnp.float32),
+            pltpu.VMEM((width // 128, 128), jnp.float32),
+            pltpu.VMEM((8, 8, 128), jnp.float32),
+            pltpu.VMEM((layers, 8, 128), jnp.float32),
             dma((6,)),
             dma((2 * layers * 3,)),
             dma((layers * 3,)),
@@ -497,13 +565,16 @@
             dma((layers * 8,)),
             dma((layers * 8,)),
             dma((layers * 8,)),
+            dma((8,)),
+            dma((8,)),
+            dma((layers,)),
+            dma((layers,)),
         ],
         compiler_params=pltpu.CompilerParams(
             collective_id=0, has_side_effects=True, vmem_limit_bytes=60 * 1024 * 1024
         ),
-    )(x, gain.reshape(1, width), codes, scales, outer.reshape(1, -1), down, up, target)
-    partial_value = jnp.sum(squares) / (tokens * fsdp * columns)
-    return kv, lax.psum(partial_value, ("grp", "fsdp"))
+    )(x, gain.reshape(-1, 128), codes, scales, outer.reshape(1, -1), down.T, up, target)
+    return kv, loss.reshape(())
 
 
 def solution(mesh):

time: 132 us -> 96.3 us (0.73)
  blocking collectives: 38.7 us -> 0 us
  Pallas kernels: 83.3 us -> 91.5 us
  local copies, waits for them, and re-layouts: 6.39 us -> 2.26 us
    psum x1 -> x0, blocking collectives: 38.7 us -> none  [per_device(): return (kv, lax.psum(partial_value, ('grp', 'fsdp')))]
    pallas_call x1, Pallas kernels: 83.3 us -> 91.5 us  [per_device(): pl.pallas_call(functools.partial(kernel, layers), out_shape=(jax.ShapeDty...]
    unnamed x2 -> x1, local copies, waits for them, and re-layouts: 5.04 us -> 2.26 us
    reshape x1 -> x0, local copies, waits for them, and re-layouts: 1.35 us -> none  [per_device(): gain.reshape(1, width)]
where the time goes in v2:
time: 96.3 us; the launch traced here: 96.1 us
  Pallas kernels  91.5 us (95%)
  between operations  2.33 us (2%)
  local copies, waits for them, and re-layouts  2.26 us (2%)
    pallas_call x1, Pallas kernels, per_device(): pl.pallas_call(functools.partial(kernel, layers), out_shape=(jax.ShapeDty...  91.5 us
    unnamed x1, local copies, waits for them, and re-layouts  2.26 us

profile of v2, /device:TPU:0, one launch (start us, length us, event | category | flops | bytes accessed | tf_op | source)
XLA Modules:
  0.0 96.1 jit_solution(3382727988560066214)
XLA Ops:
  0.6 91.5 %shard_map.95 = (bf16[512,1024]{1,0:T(8,128)(2,1)}, f32[1,1]{1,0:T(1,128)}) custom-call(bf16[512,8192]{1,0:T(8,128)(2,1)} %x_hbm.1, bf16[64,128]{1,0:T(8,128)(2,1)} %bitcast.5, s32[1024,256]{1,0:T(8,128)} %codes_ref.1, s32[32,128]{1,0:T(8,128)} %scales_ref.1, s32[1,64]{1,0:T(1,128)} %bitcast.6, bf16[64,8192]{1,0:T(8,128)(2,1)} %bitcast.4, ...), custom_call_target="tpu_custom_call" | custom-call | tf_op jit(solution)/shard_map/pallas_call | solution.py:541
  92.1 2.3 %copy.12 = bf16[512,1024]{1,0:T(8,128)(2,1)} copy(bf16[512,1024]{1,0:T(8,128)(2,1)} %get-tuple-element.8) | data formatting | bytes 2097152

commit v3 on v2

--- a/solution.py
+++ b/solution.py
@@ -386,13 +386,16 @@
         arrived(cl, 1 - cy, q)
         core_copy(cl, 1 - cy, q).start()
 
+    def late(s):
+        pl.when(s <= 4)(lambda: own_event(s - 1))
+        xy_event(s - 1, 0)
+        xy_event(s - 1, 1)
+
     def one_step(s, carry):
         z_event(s, 0)
-        pl.when(s <= 4)(lambda: own_event(s - 1))
 
         @pl.when(s > 1)
         def _():
-            xy_event(s - 1, 1)
             both(s - 1, lambda layer, step: multiply_arrived(layer, cy))
 
         @pl.when(s == 1)
@@ -402,11 +405,8 @@
 
         z_event(s, 1)
         y_event(s, 0)
-        xz_event(s)
-
-        @pl.when(s > 1)
-        def _():
-            both(s - 1, lambda layer, step: multiply_arrived(layer, 1 - cy))
+        pl.when(s > 1)(lambda: late(s))
+        pl.when(s == 1)(lambda: own_event(0))
 
         @pl.when(s == 1)
         def _():
@@ -416,7 +416,11 @@
         z_event(s, 2)
         pl.when(s < 4)(lambda: own_copy(s).start())
         y_event(s, 1)
-        xy_event(s, 0)
+        xz_event(s)
+
+        @pl.when(s > 1)
+        def _():
+            both(s - 1, lambda layer, step: multiply_arrived(layer, 1 - cy))
 
         @pl.when(s == 1)
         def _():
@@ -426,6 +430,7 @@
         return carry
 
     lax.fori_loop(1, layers, one_step, 0)
+    xy_event(layers - 1, 0)
     both(layers - 1, lambda layer, step: multiply_arrived(layer, cy))
     for k in range(min(layers - 1, 4), 4):
         own_event(k)

time: 96.3 us -> 90.1 us (0.936)
  Pallas kernels: 91.5 us -> 85.3 us
    pallas_call x1, Pallas kernels: 91.5 us -> 85.3 us  [per_device(): pl.pallas_call(functools.partial(kernel, layers), out_shape=(jax.ShapeDty...]
where the time goes in v3:
time: 90.1 us; the launch traced here: 89.9 us
  Pallas kernels  85.3 us (95%)
  between operations  2.33 us (3%)
  local copies, waits for them, and re-layouts  2.26 us (3%)
    pallas_call x1, Pallas kernels, per_device(): pl.pallas_call(functools.partial(kernel, layers), out_shape=(jax.ShapeDty...  85.3 us
    unnamed x1, local copies, waits for them, and re-layouts  2.26 us

profile of v3, /device:TPU:0, one launch (start us, length us, event | category | flops | bytes accessed | tf_op | source)
XLA Modules:
  0.0 89.9 jit_solution(4152651085852061197)
XLA Ops:
  0.6 85.3 %shard_map.95 = (bf16[512,1024]{1,0:T(8,128)(2,1)}, f32[1,1]{1,0:T(1,128)}) custom-call(bf16[512,8192]{1,0:T(8,128)(2,1)} %x_hbm.1, bf16[64,128]{1,0:T(8,128)(2,1)} %bitcast.5, s32[1024,256]{1,0:T(8,128)} %codes_ref.1, s32[32,128]{1,0:T(8,128)} %scales_ref.1, s32[1,64]{1,0:T(1,128)} %bitcast.6, bf16[64,8192]{1,0:T(8,128)(2,1)} %bitcast.4, ...), custom_call_target="tpu_custom_call" | custom-call | tf_op jit(solution)/shard_map/pallas_call | solution.py:546
  85.9 2.3 %copy.12 = bf16[512,1024]{1,0:T(8,128)(2,1)} copy(bf16[512,1024]{1,0:T(8,128)(2,1)} %get-tuple-element.8) | data formatting | bytes 2097152
